TPU v7x, 512 devices: a whole 4x8x8 slice. The times are simulated.
512 devices in a mesh: rows: 128 (over x_hi, z, y), feat: 4 (over x_lo, core).
Axes of the slice: x: 4 (x_hi: 2, x_lo: 2; x = x_hi * 2 + x_lo), y: 8, z: 8, core: 2. Of those that a mesh axis runs over, the one named last changes fastest.
Arguments:
- features: bfloat16 [131072, 64], P('rows', 'feat'), may hold values from -0.75 to 0.75
- probes: bfloat16 [131072, 32], P('rows', 'feat'), may hold values from -6 to 6
- theta: float32 [1], replicated, may hold values from 0.18 to 0.69
- block_mask: int32 [128, 9], P('rows'), may hold values 0 or 1
- order: int32 [128, 1024], P('rows'), may hold values from 0 to 1023, each once within a row
Outputs:
- kernel_probes: float32 [131072, 32], P('rows', 'feat')
- deriv_probes: float32 [131072, 32], P('rows', 'feat')
All inputs are finite; a program needn't handle non-finite values. No bound on the sum of `block_mask` on one device may be relied on, other than what follows from the above.
Results may differ from a plain program's by a relative error of at most 0.003.
Values may be sent and summed in bfloat16 or wider, within the bound.
A program may use at most 64 MiB of HBM per device.

v0:
```python
import jax
import jax.numpy as jnp
from jax import lax
from jax.sharding import PartitionSpec as P


def sent_to_all(value, axis):
    copies = jnp.broadcast_to(value, (lax.axis_size(axis), *value.shape))
    return lax.all_to_all(copies, axis, split_axis=0, concat_axis=0, tiled=True)


def in_order(tiles, dim):
    shape = list(tiles.shape[1:])
    shape[dim] *= tiles.shape[0]
    return jnp.moveaxis(tiles, 0, dim).reshape(shape)


def collect(value, axis, dim):
    tiles = sent_to_all(value, axis)
    return in_order(tiles, dim)


def passed_along(value, axis, steps):
    count = lax.axis_size(axis)
    pairs = [(source, (source + steps) % count) for source in range(count)]
    return lax.ppermute(value, axis, pairs)


def split_up(value, dim, devices):
    shape = value.shape
    tiles = value.reshape(*shape[:dim], devices, shape[dim] // devices, *shape[dim + 1 :])
    return jnp.moveaxis(tiles, dim, 0)


def sent_and_summed(value, axis, dim):
    tiles = split_up(value, dim, lax.axis_size(axis))
    arrived = lax.all_to_all(tiles, axis, split_axis=0, concat_axis=0, tiled=True)
    return arrived.sum(axis=0)


def sent_together(arrays, axis, dim, along):
    widths = [a.shape[along] for a in arrays]
    both = jnp.concatenate(arrays, axis=along)
    out = sent_and_summed(both, axis, dim)
    return tuple(jnp.split(out, [sum(widths[:k]) for k in range(1, len(widths))], axis=along))


def body(features, probes, theta, block_mask, order):
    own_full = lax.all_gather(features, "feat", axis=1, tiled=True)
    scale = jnp.exp(-2.0 * theta[0])
    own_sq = jnp.sum(own_full.astype(jnp.float32) ** 2, axis=1)
    rows_here = probes.shape[0]

    def tile_terms(panel_full, panel_probes, active):
        panel_sq = jnp.sum(panel_full.astype(jnp.float32) ** 2, axis=1)
        cross = lax.dot_general(
            own_full, panel_full, (((1,), (1,)), ((), ())), preferred_element_type=jnp.float32
        )
        dist2 = jnp.maximum(own_sq[:, None] + panel_sq[None, :] - 2.0 * cross, 0.0)
        radius2 = dist2 * scale
        radius = jnp.sqrt(radius2)
        inside = jnp.maximum(1.0 - radius, 0.0)
        inside2 = inside * inside
        kern = (inside2 * inside2 * (4.0 * radius + 1.0)).astype(jnp.bfloat16)
        deriv = (20.0 * radius2 * inside2 * inside).astype(jnp.bfloat16)
        first = jnp.dot(kern, panel_probes, preferred_element_type=jnp.float32)
        second = jnp.dot(deriv, panel_probes, preferred_element_type=jnp.float32)
        weight = (active > 0).astype(jnp.float32)
        return (first * weight, second * weight)

    all_probes = collect(probes, "feat", 1)
    ordered_all = jnp.take(all_probes, order[0], axis=0)
    quarter = rows_here // lax.axis_size("feat")
    start = lax.axis_index("feat") * quarter
    carried = lax.dynamic_slice_in_dim(own_full, start, quarter, 0)
    panel_probes = lax.dynamic_slice_in_dim(ordered_all, start, quarter, 0)
    total_k, total_d = tile_terms(carried, panel_probes, jnp.int32(1))
    upper = (carried, panel_probes)
    lower = (carried, panel_probes)
    for step in range(1, 5):
        upper = passed_along((upper[0], upper[1]), "rows", -1)
        lower = passed_along((lower[0], lower[1]), "rows", 1)
        add_k, add_d = tile_terms(upper[0], upper[1], block_mask[0, 4 + step])
        total_k, total_d = (total_k + add_k, total_d + add_d)
        add_k, add_d = tile_terms(lower[0], lower[1], block_mask[0, 4 - step])
        total_k, total_d = (total_k + add_k, total_d + add_d)
    total_k, total_d = sent_together((total_k, total_d), "feat", 1, 0)
    return (total_k, total_d)


def solution(mesh):
    return jax.shard_map(
        body,
        mesh=mesh,
        in_specs=(P("rows", "feat"), P("rows", "feat"), P(), P("rows", None), P("rows", None)),
        out_specs=(P("rows", "feat"), P("rows", "feat")),
        check_vma=False,
    )
```

profile of v0, /device:TPU:1, one launch (start us, length us, event | category | flops | bytes accessed | tf_op | source)
XLA Modules:
  0.0 137.9 jit_solution(5949143357094899956)
XLA Ops:
  0.6 12.3 %all_gather.3 = bf16[1024,64]{0,1:T(8,128)(2,1)S(1)} all-gather(bf16[1024,16]{0,1:T(8,128)(2,1)} %param.5), channel_id=1, replica_groups=mesh['rows'=128,'feat'=4] {'feat'}, dimensions={1}, use_global_device_ids=true | all-gather | bytes 163840 | tf_op jit(solution)/shard_map/all_gather | solution.py:49
  13.0 10.7 %collective-permute-start = (bf16[256,64]{0,1:T(8,128)(2,1)S(1)}, bf16[256,64]{0,1:T(8,128)(2,1)S(1)}, u32[]{:S(2)}, u32[]{:S(2)}) collective-permute-start(bf16[256,64]{0,1:T(8,128)(2,1)S(1)} %get-tuple-element.3), channel_id=1, source_target_pairs={{0,508},{4,0},{8,4},{12,8},{16,12},{20,16},{24,20},{28,24},{32,28}... | collective-permute-start | bytes 98312 | tf_op jit(solution)/shard_map/ppermute | solution.py:26
  23.7 1.9 %collective-permute-start.2 = (bf16[256,64]{0,1:T(8,128)(2,1)S(1)}, bf16[256,64]{0,1:T(8,128)(2,1)S(1)}, u32[]{:S(2)}, u32[]{:S(2)}) collective-permute-start(bf16[256,64]{0,1:T(8,128)(2,1)S(1)} %get-tuple-element.3), channel_id=1, source_target_pairs={{0,4},{4,8},{8,12},{12,16},{16,20},{20,24},{24,28},{28,32},{32,36}... | collective-permute-start | bytes 98312 | tf_op jit(solution)/shard_map/ppermute | solution.py:26
  26.2 3.7 %all-to-all-start = ((bf16[4,1024,8]{1,2,0:T(8,128)(2,1)}), bf16[4,1024,8]{1,2,0:T(8,128)(2,1)S(1)}, u32[]{:S(2)}, u32[]{:S(2)}) async-start(bf16[4,1024,8]{1,2,0:T(8,128)(2,1)} %broadcast_in_dim.13), calls=%async_computation | async-start | bytes 131072 | tf_op jit(solution)/shard_map/all_to_all | solution.py:9
  30.7 1.3 fusion.11
  37.9 9.4 %collective-permute-start.4 = (bf16[256,64]{0,1:T(8,128)(2,1)S(1)}, bf16[256,64]{0,1:T(8,128)(2,1)S(1)}, u32[]{:S(2)}, u32[]{:S(2)}) collective-permute-start(bf16[256,64]{0,1:T(8,128)(2,1)S(1)} %collective-permute-done), channel_id=1, source_target_pairs={{0,508},{4,0},{8,4},{12,8},{16,12},{20,16},{24,20},{28,24},{32,28}... | collective-permute-start | bytes 98312 | tf_op jit(solution)/shard_map/ppermute | solution.py:26
  47.3 1.9 %collective-permute-start.6 = (bf16[256,64]{0,1:T(8,128)(2,1)S(1)}, bf16[256,64]{0,1:T(8,128)(2,1)S(1)}, u32[]{:S(2)}, u32[]{:S(2)}) collective-permute-start(bf16[256,64]{0,1:T(8,128)(2,1)S(1)} %collective-permute-done.2), channel_id=1, source_target_pairs={{0,4},{4,8},{8,12},{12,16},{16,20},{20,24},{24,28},{28,32},{32,36}... | collective-permute-start | bytes 98312 | tf_op jit(solution)/shard_map/ppermute | solution.py:26
  50.1 3.2 %gather_fusion = bf16[1024,32]{1,0:T(8,128)(2,1)S(1)} fusion(bf16[1024,32]{1,0:T(8,128)(2,1)S(1)} %copy.8, s32[1024]{0:T(1024)S(1)} %broadcast_clamp_fusion), kind=kCustom, calls=%fused_computation | custom fusion | bytes 135168 | tf_op jit(solution)/shard_map/jit(_take)/gather | solution.py:72
  53.4 2.1 %collective-permute-start.3 = (bf16[256,32]{1,0:T(8,128)(2,1)S(1)}, bf16[256,32]{1,0:T(8,128)(2,1)S(1)}, u32[]{:S(2)}, u32[]{:S(2)}) collective-permute-start(bf16[256,32]{1,0:T(8,128)(2,1)S(1)} %dynamic-slice_select_fusion), channel_id=1, source_target_pairs={{0,4},{4,8},{8,12},{12,16},{16,20},{20,24},{24,28},{28,32},{32,36}... | collective-permute-start | bytes 49160 | tf_op jit(solution)/shard_map/ppermute | solution.py:26
  55.5 9.1 %collective-permute-start.1 = (bf16[256,32]{1,0:T(8,128)(2,1)S(1)}, bf16[256,32]{1,0:T(8,128)(2,1)S(1)}, u32[]{:S(2)}, u32[]{:S(2)}) collective-permute-start(bf16[256,32]{1,0:T(8,128)(2,1)S(1)} %dynamic-slice_select_fusion), channel_id=1, source_target_pairs={{0,508},{4,0},{8,4},{12,8},{16,12},{20,16},{24,20},{28,24},{32,28}... | collective-permute-start | bytes 49160 | tf_op jit(solution)/shard_map/ppermute | solution.py:26
  64.5 1.8 %fusion.28 = f32[1024,32]{0,1:T(8,128)S(1)} fusion(bf16[256,32]{1,0:T(8,128)(2,1)S(1)} %dynamic-slice_select_fusion, f32[1024,256]{0,1:T(8,128)} %fusion.11), kind=kOutput, calls=%fused_computation.89 | convolution fusion | flops 18612224 | bytes 1196032 | tf_op jit(solution)/shard_map/dot_general | solution.py:67
  67.0 3.4 %collective-permute-start.8 = (bf16[256,64]{0,1:T(8,128)(2,1)S(1)}, bf16[256,64]{0,1:T(8,128)(2,1)S(1)}, u32[]{:S(2)}, u32[]{:S(2)}) collective-permute-start(bf16[256,64]{0,1:T(8,128)(2,1)S(1)} %collective-permute-done.4), channel_id=1, source_target_pairs={{0,508},{4,0},{8,4},{12,8},{16,12},{20,16},{24,20},{28,24},{32,28}... | collective-permute-start | bytes 98312 | tf_op jit(solution)/shard_map/ppermute | solution.py:26
  70.4 1.9 %collective-permute-start.10 = (bf16[256,64]{0,1:T(8,128)(2,1)S(1)}, bf16[256,64]{0,1:T(8,128)(2,1)S(1)}, u32[]{:S(2)}, u32[]{:S(2)}) collective-permute-start(bf16[256,64]{0,1:T(8,128)(2,1)S(1)} %collective-permute-done.6), channel_id=1, source_target_pairs={{0,4},{4,8},{8,12},{12,16},{16,20},{20,24},{24,28},{28,32},{32,36}... | collective-permute-start | bytes 98312 | tf_op jit(solution)/shard_map/ppermute | solution.py:26
  73.0 1.9 %collective-permute-start.7 = (bf16[256,32]{1,0:T(8,128)(2,1)S(1)}, bf16[256,32]{1,0:T(8,128)(2,1)S(1)}, u32[]{:S(2)}, u32[]{:S(2)}) collective-permute-start(bf16[256,32]{1,0:T(8,128)(2,1)S(1)} %collective-permute-done.3), channel_id=1, source_target_pairs={{0,4},{4,8},{8,12},{12,16},{16,20},{20,24},{24,28},{28,32},{32,36}... | collective-permute-start | bytes 49160 | tf_op jit(solution)/shard_map/ppermute | solution.py:26
  74.9 9.1 %collective-permute-start.5 = (bf16[256,32]{1,0:T(8,128)(2,1)S(1)}, bf16[256,32]{1,0:T(8,128)(2,1)S(1)}, u32[]{:S(2)}, u32[]{:S(2)}) collective-permute-start(bf16[256,32]{1,0:T(8,128)(2,1)S(1)} %collective-permute-done.1), channel_id=1, source_target_pairs={{0,508},{4,0},{8,4},{12,8},{16,12},{20,16},{24,20},{28,24},{32,28}... | collective-permute-start | bytes 49160 | tf_op jit(solution)/shard_map/ppermute | solution.py:26
  84.0 0.8 fusion.19
  84.8 0.8 fusion.27
  85.7 0.8 fusion.26
  87.3 1.9 %collective-permute-start.11 = (bf16[256,32]{1,0:T(8,128)(2,1)S(1)}, bf16[256,32]{1,0:T(8,128)(2,1)S(1)}, u32[]{:S(2)}, u32[]{:S(2)}) collective-permute-start(bf16[256,32]{1,0:T(8,128)(2,1)S(1)} %collective-permute-done.7), channel_id=1, source_target_pairs={{0,4},{4,8},{8,12},{12,16},{16,20},{20,24},{24,28},{28,32},{32,36}... | collective-permute-start | bytes 49160 | tf_op jit(solution)/shard_map/ppermute | solution.py:26
  90.1 0.8 convolution_multiply_fusion.21
  90.9 9.1 %collective-permute-start.9 = (bf16[256,32]{1,0:T(8,128)(2,1)S(1)}, bf16[256,32]{1,0:T(8,128)(2,1)S(1)}, u32[]{:S(2)}, u32[]{:S(2)}) collective-permute-start(bf16[256,32]{1,0:T(8,128)(2,1)S(1)} %collective-permute-done.5), channel_id=1, source_target_pairs={{0,508},{4,0},{8,4},{12,8},{16,12},{20,16},{24,20},{28,24},{32,28}... | collective-permute-start | bytes 49160 | tf_op jit(solution)/shard_map/ppermute | solution.py:26
  100.8 0.8 fusion.25
  101.7 1.9 %collective-permute-start.12 = (bf16[256,64]{0,1:T(8,128)(2,1)S(1)}, bf16[256,64]{0,1:T(8,128)(2,1)S(1)}, u32[]{:S(2)}, u32[]{:S(2)}) collective-permute-start(bf16[256,64]{0,1:T(8,128)(2,1)S(1)} %collective-permute-done.8), channel_id=1, source_target_pairs={{0,508},{4,0},{8,4},{12,8},{16,12},{20,16},{24,20},{28,24},{32,28}... | collective-permute-start | bytes 98312 | tf_op jit(solution)/shard_map/ppermute | solution.py:26
  103.6 3.4 %collective-permute-start.14 = (bf16[256,64]{0,1:T(8,128)(2,1)S(1)}, bf16[256,64]{0,1:T(8,128)(2,1)S(1)}, u32[]{:S(2)}, u32[]{:S(2)}) collective-permute-start(bf16[256,64]{0,1:T(8,128)(2,1)S(1)} %collective-permute-done.10), channel_id=1, source_target_pairs={{0,4},{4,8},{8,12},{12,16},{16,20},{20,24},{24,28},{28,32},{32,36}... | collective-permute-start | bytes 98312 | tf_op jit(solution)/shard_map/ppermute | solution.py:26
  107.7 1.9 %collective-permute-start.15 = (bf16[256,32]{1,0:T(8,128)(2,1)S(1)}, bf16[256,32]{1,0:T(8,128)(2,1)S(1)}, u32[]{:S(2)}, u32[]{:S(2)}) collective-permute-start(bf16[256,32]{1,0:T(8,128)(2,1)S(1)} %collective-permute-done.11), channel_id=1, source_target_pairs={{0,4},{4,8},{8,12},{12,16},{16,20},{20,24},{24,28},{28,32},{32,36}... | collective-permute-start | bytes 49160 | tf_op jit(solution)/shard_map/ppermute | solution.py:26
  110.4 0.8 convolution_multiply_fusion.19
  111.2 9.3 %collective-permute-start.13 = (bf16[256,32]{1,0:T(8,128)(2,1)S(1)}, bf16[256,32]{1,0:T(8,128)(2,1)S(1)}, u32[]{:S(2)}, u32[]{:S(2)}) collective-permute-start(bf16[256,32]{1,0:T(8,128)(2,1)S(1)} %collective-permute-done.9), channel_id=1, source_target_pairs={{0,508},{4,0},{8,4},{12,8},{16,12},{20,16},{24,20},{28,24},{32,28}... | collective-permute-start | bytes 49160 | tf_op jit(solution)/shard_map/ppermute | solution.py:26
  120.5 0.8 fusion.23
  121.3 0.8 fusion.15
  123.3 0.8 convolution_multiply_fusion.17
  125.3 0.8 fusion.21
  126.2 11.1 %all_to_all.10 = f32[4,2048,8]{1,2,0:T(8,128)S(1)} all-to-all(f32[4,2048,8]{1,2,0:T(8,128)S(1)} %maximum_bitcast_fusion), channel_id=1, replica_groups=mesh['rows'=128,'feat'=4] {'feat'}, dimensions={0} | all-to-all | bytes 524288 | tf_op jit(solution)/shard_map/all_to_all | solution.py:37
  (61 shorter events, 10.6 us)
Async XLA Ops:
  12.9 12.7 %copy-start.1 = (bf16[1024,8]{0,1:T(8,128)(2,1)S(1)}, bf16[1024,8]{0,1:T(8,128)(2,1)}, u32[]{:S(2)}) copy-start(bf16[1024,8]{0,1:T(8,128)(2,1)} %param.6) | copy-start | bytes 49156
  13.0 24.9 %collective-permute-start = (bf16[256,64]{0,1:T(8,128)(2,1)S(1)}, bf16[256,64]{0,1:T(8,128)(2,1)S(1)}, u32[]{:S(2)}, u32[]{:S(2)}) collective-permute-start(bf16[256,64]{0,1:T(8,128)(2,1)S(1)} %get-tuple-element.3), channel_id=1, source_target_pairs={{0,508},{4,0},{8,4},{12,8},{16,12},{20,16},{24,20},{28,24},{32,28}... | collective-permute-start | bytes 98312 | tf_op jit(solution)/shard_map/ppermute | solution.py:26
  23.7 23.6 %collective-permute-start.2 = (bf16[256,64]{0,1:T(8,128)(2,1)S(1)}, bf16[256,64]{0,1:T(8,128)(2,1)S(1)}, u32[]{:S(2)}, u32[]{:S(2)}) collective-permute-start(bf16[256,64]{0,1:T(8,128)(2,1)S(1)} %get-tuple-element.3), channel_id=1, source_target_pairs={{0,4},{4,8},{8,12},{12,16},{16,20},{20,24},{24,28},{28,32},{32,36}... | collective-permute-start | bytes 98312 | tf_op jit(solution)/shard_map/ppermute | solution.py:26
  26.2 23.6 %all-to-all-start = ((bf16[4,1024,8]{1,2,0:T(8,128)(2,1)}), bf16[4,1024,8]{1,2,0:T(8,128)(2,1)S(1)}, u32[]{:S(2)}, u32[]{:S(2)}) async-start(bf16[4,1024,8]{1,2,0:T(8,128)(2,1)} %broadcast_in_dim.13), calls=%async_computation | async-start | bytes 131072 | tf_op jit(solution)/shard_map/all_to_all | solution.py:9
  30.0 0.7 copy-start.2
  30.7 1.4 copy-start
  37.9 29.1 %collective-permute-start.4 = (bf16[256,64]{0,1:T(8,128)(2,1)S(1)}, bf16[256,64]{0,1:T(8,128)(2,1)S(1)}, u32[]{:S(2)}, u32[]{:S(2)}) collective-permute-start(bf16[256,64]{0,1:T(8,128)(2,1)S(1)} %collective-permute-done), channel_id=1, source_target_pairs={{0,508},{4,0},{8,4},{12,8},{16,12},{20,16},{24,20},{28,24},{32,28}... | collective-permute-start | bytes 98312 | tf_op jit(solution)/shard_map/ppermute | solution.py:26
  47.3 23.1 %collective-permute-start.6 = (bf16[256,64]{0,1:T(8,128)(2,1)S(1)}, bf16[256,64]{0,1:T(8,128)(2,1)S(1)}, u32[]{:S(2)}, u32[]{:S(2)}) collective-permute-start(bf16[256,64]{0,1:T(8,128)(2,1)S(1)} %collective-permute-done.2), channel_id=1, source_target_pairs={{0,4},{4,8},{8,12},{12,16},{16,20},{20,24},{24,28},{28,32},{32,36}... | collective-permute-start | bytes 98312 | tf_op jit(solution)/shard_map/ppermute | solution.py:26
  53.3 13.1 %copy-start.3 = (f32[1024,256]{0,1:T(8,128)S(1)}, f32[1024,256]{0,1:T(8,128)}, u32[]{:S(2)}) copy-start(f32[1024,256]{0,1:T(8,128)} %fusion.11) | copy-start | bytes 3145732
  53.4 19.6 %collective-permute-start.3 = (bf16[256,32]{1,0:T(8,128)(2,1)S(1)}, bf16[256,32]{1,0:T(8,128)(2,1)S(1)}, u32[]{:S(2)}, u32[]{:S(2)}) collective-permute-start(bf16[256,32]{1,0:T(8,128)(2,1)S(1)} %dynamic-slice_select_fusion), channel_id=1, source_target_pairs={{0,4},{4,8},{8,12},{12,16},{16,20},{20,24},{24,28},{28,32},{32,36}... | collective-permute-start | bytes 49160 | tf_op jit(solution)/shard_map/ppermute | solution.py:26
  55.5 19.5 %collective-permute-start.1 = (bf16[256,32]{1,0:T(8,128)(2,1)S(1)}, bf16[256,32]{1,0:T(8,128)(2,1)S(1)}, u32[]{:S(2)}, u32[]{:S(2)}) collective-permute-start(bf16[256,32]{1,0:T(8,128)(2,1)S(1)} %dynamic-slice_select_fusion), channel_id=1, source_target_pairs={{0,508},{4,0},{8,4},{12,8},{16,12},{20,16},{24,20},{28,24},{32,28}... | collective-permute-start | bytes 49160 | tf_op jit(solution)/shard_map/ppermute | solution.py:26
  67.0 34.6 %collective-permute-start.8 = (bf16[256,64]{0,1:T(8,128)(2,1)S(1)}, bf16[256,64]{0,1:T(8,128)(2,1)S(1)}, u32[]{:S(2)}, u32[]{:S(2)}) collective-permute-start(bf16[256,64]{0,1:T(8,128)(2,1)S(1)} %collective-permute-done.4), channel_id=1, source_target_pairs={{0,508},{4,0},{8,4},{12,8},{16,12},{20,16},{24,20},{28,24},{32,28}... | collective-permute-start | bytes 98312 | tf_op jit(solution)/shard_map/ppermute | solution.py:26
  70.4 33.2 %collective-permute-start.10 = (bf16[256,64]{0,1:T(8,128)(2,1)S(1)}, bf16[256,64]{0,1:T(8,128)(2,1)S(1)}, u32[]{:S(2)}, u32[]{:S(2)}) collective-permute-start(bf16[256,64]{0,1:T(8,128)(2,1)S(1)} %collective-permute-done.6), channel_id=1, source_target_pairs={{0,4},{4,8},{8,12},{12,16},{16,20},{20,24},{24,28},{28,32},{32,36}... | collective-permute-start | bytes 98312 | tf_op jit(solution)/shard_map/ppermute | solution.py:26
  73.0 14.3 %collective-permute-start.7 = (bf16[256,32]{1,0:T(8,128)(2,1)S(1)}, bf16[256,32]{1,0:T(8,128)(2,1)S(1)}, u32[]{:S(2)}, u32[]{:S(2)}) collective-permute-start(bf16[256,32]{1,0:T(8,128)(2,1)S(1)} %collective-permute-done.3), channel_id=1, source_target_pairs={{0,4},{4,8},{8,12},{12,16},{16,20},{20,24},{24,28},{28,32},{32,36}... | collective-permute-start | bytes 49160 | tf_op jit(solution)/shard_map/ppermute | solution.py:26
  74.9 16.0 %collective-permute-start.5 = (bf16[256,32]{1,0:T(8,128)(2,1)S(1)}, bf16[256,32]{1,0:T(8,128)(2,1)S(1)}, u32[]{:S(2)}, u32[]{:S(2)}) collective-permute-start(bf16[256,32]{1,0:T(8,128)(2,1)S(1)} %collective-permute-done.1), channel_id=1, source_target_pairs={{0,508},{4,0},{8,4},{12,8},{16,12},{20,16},{24,20},{28,24},{32,28}... | collective-permute-start | bytes 49160 | tf_op jit(solution)/shard_map/ppermute | solution.py:26
  87.3 20.3 %collective-permute-start.11 = (bf16[256,32]{1,0:T(8,128)(2,1)S(1)}, bf16[256,32]{1,0:T(8,128)(2,1)S(1)}, u32[]{:S(2)}, u32[]{:S(2)}) collective-permute-start(bf16[256,32]{1,0:T(8,128)(2,1)S(1)} %collective-permute-done.7), channel_id=1, source_target_pairs={{0,4},{4,8},{8,12},{12,16},{16,20},{20,24},{24,28},{28,32},{32,36}... | collective-permute-start | bytes 49160 | tf_op jit(solution)/shard_map/ppermute | solution.py:26
  90.9 20.3 %collective-permute-start.9 = (bf16[256,32]{1,0:T(8,128)(2,1)S(1)}, bf16[256,32]{1,0:T(8,128)(2,1)S(1)}, u32[]{:S(2)}, u32[]{:S(2)}) collective-permute-start(bf16[256,32]{1,0:T(8,128)(2,1)S(1)} %collective-permute-done.5), channel_id=1, source_target_pairs={{0,508},{4,0},{8,4},{12,8},{16,12},{20,16},{24,20},{28,24},{32,28}... | collective-permute-start | bytes 49160 | tf_op jit(solution)/shard_map/ppermute | solution.py:26
  101.7 22.5 %collective-permute-start.12 = (bf16[256,64]{0,1:T(8,128)(2,1)S(1)}, bf16[256,64]{0,1:T(8,128)(2,1)S(1)}, u32[]{:S(2)}, u32[]{:S(2)}) collective-permute-start(bf16[256,64]{0,1:T(8,128)(2,1)S(1)} %collective-permute-done.8), channel_id=1, source_target_pairs={{0,508},{4,0},{8,4},{12,8},{16,12},{20,16},{24,20},{28,24},{32,28}... | collective-permute-start | bytes 98312 | tf_op jit(solution)/shard_map/ppermute | solution.py:26
  103.6 18.5 %collective-permute-start.14 = (bf16[256,64]{0,1:T(8,128)(2,1)S(1)}, bf16[256,64]{0,1:T(8,128)(2,1)S(1)}, u32[]{:S(2)}, u32[]{:S(2)}) collective-permute-start(bf16[256,64]{0,1:T(8,128)(2,1)S(1)} %collective-permute-done.10), channel_id=1, source_target_pairs={{0,4},{4,8},{8,12},{12,16},{16,20},{20,24},{24,28},{28,32},{32,36}... | collective-permute-start | bytes 98312 | tf_op jit(solution)/shard_map/ppermute | solution.py:26
  107.7 14.8 %collective-permute-start.15 = (bf16[256,32]{1,0:T(8,128)(2,1)S(1)}, bf16[256,32]{1,0:T(8,128)(2,1)S(1)}, u32[]{:S(2)}, u32[]{:S(2)}) collective-permute-start(bf16[256,32]{1,0:T(8,128)(2,1)S(1)} %collective-permute-done.11), channel_id=1, source_target_pairs={{0,4},{4,8},{8,12},{12,16},{16,20},{20,24},{24,28},{28,32},{32,36}... | collective-permute-start | bytes 49160 | tf_op jit(solution)/shard_map/ppermute | solution.py:26
  111.2 13.3 %collective-permute-start.13 = (bf16[256,32]{1,0:T(8,128)(2,1)S(1)}, bf16[256,32]{1,0:T(8,128)(2,1)S(1)}, u32[]{:S(2)}, u32[]{:S(2)}) collective-permute-start(bf16[256,32]{1,0:T(8,128)(2,1)S(1)} %collective-permute-done.9), channel_id=1, source_target_pairs={{0,508},{4,0},{8,4},{12,8},{16,12},{20,16},{24,20},{28,24},{32,28}... | collective-permute-start | bytes 49160 | tf_op jit(solution)/shard_map/ppermute | solution.py:26
where the time goes:
time: 139 us; the launch traced here: 138 us
  starting transfers between devices  82.5 us (59%)
  blocking collectives  23.4 us (17%)
  matrix products  19.2 us (14%)
  between operations  6.92 us (5%)
  local copies, waits for them, and re-layouts  5.4 us (4%)
    ppermute x16, starting transfers between devices, passed_along(): return lax.ppermute(value, axis, pairs)  78.8 us
    all_gather x1, blocking collectives, body(): own_full = lax.all_gather(features, 'feat', axis=1, tiled=True)  12.3 us
    all_to_all x1, blocking collectives, sent_and_summed(): lax.all_to_all(tiles, axis, split_axis=0, concat_axis=0, tiled=True)  11.1 us
    dot_general x9, matrix products, tile_terms(): second = jnp.dot(deriv, panel_probes, preferred_element_type=jnp.float32)  8.17 us
    dot_general x9, matrix products, tile_terms(): first = jnp.dot(kern, panel_probes, preferred_element_type=jnp.float32)  7.21 us
    dot_general x9, matrix products, tile_terms(): lax.dot_general(own_full, panel_full, (((1,), (1,)), ((), ())), preferred...  3.86 us
    all_to_all x1, starting transfers between devices, sent_to_all(): return lax.all_to_all(copies, axis, split_axis=0, concat_axis=0, tiled=True)  3.69 us
    gather x1, local copies, waits for them, and re-layouts, body(): ordered_all = jnp.take(all_probes, order[0], axis=0)  3.21 us
  transfers between devices with their start and end apart: 17, of which 0 were waited for; matrix products, arithmetic and copies ran while one was open for 16% of the time, Pallas kernels for 0%

commit v1 on v0

v1 whole, which is shorter than its diff:
```python
import functools

import jax
import jax.numpy as jnp
from jax import lax
from jax.experimental import pallas as pl
from jax.experimental.pallas import tpu as pltpu
from jax.sharding import PartitionSpec as P

MESH = pl.DeviceIdType.MESH
BF = jnp.bfloat16
F32 = jnp.float32
ROUTE = {1: 1, 2: 2, 3: 1, 4: 2}
OFFS = (1, -1, 2, -2, 3, -3, 4, -4)
SLOT = {k: i for i, k in enumerate(OFFS)}
DIRECT = [k for k in OFFS if ROUTE[abs(k)] == abs(k)]
TINY = 1e-30


def rounded(value):
    return value.astype(BF).astype(F32)


def split3(value):
    high = rounded(value)
    rest = value - high
    middle = rounded(rest)
    return high, middle, rest - middle


def stacked_rows(rows, width):
    index = lax.broadcasted_iota(jnp.int32, (8, width), 0)
    out = jnp.zeros((8, width), F32)
    for place, row in enumerate(rows):
        out = jnp.where(index == place, row, out)
    return out


def kernel(
    blocks, feats, ft, pt, theta, mask, order, out_k, out_d,
    own, raw, order_v, full, own_z, slots, right, acc_k, acc_d, out_s, out_r,
    load_sem, full_send, full_recv, z_send, z_recv, slot_send, slot_recv, red_send, red_recv,
):
    row = lax.axis_index("rows")
    col = lax.axis_index("feat")
    points = own.shape[2]
    panel = points // feats
    width = panel

    def at(step):
        return lax.rem(row + step + blocks, blocks)

    def device(step, other):
        return (at(step), other)

    def peer(i):
        return lax.rem(col + i, feats)

    barrier = pltpu.get_barrier_semaphore()
    greeted = 0
    for i in range(1, feats):
        pl.semaphore_signal(barrier, inc=1, device_id=(row, peer(i)), device_id_type=MESH)
        greeted += 1
    reach = sorted({s * ROUTE[abs(k)] for k in OFFS for s in (1, -1)}, key=abs)
    for step in reach:
        for other in range(feats):
            pl.semaphore_signal(barrier, inc=1, device_id=device(step, other), device_id_type=MESH)
            greeted += 1

    loads = [
        pltpu.make_async_copy(order, order_v, load_sem.at[0]),
        pltpu.make_async_copy(pt, raw, load_sem.at[1]),
        pltpu.make_async_copy(ft, own.at[0:2], load_sem.at[2]),
        pltpu.make_async_copy(ft, full.at[col], load_sem.at[3]),
    ]
    for load in loads:
        load.start()

    scale16 = 16.0 * jnp.exp(jnp.full((1, panel), -2.0 * theta[0], F32))

    loads[0].wait()
    loads[1].wait()
    wanted = order_v[...]
    ordered = jnp.zeros((8, points), F32)
    for part in range(points // panel):
        source = lax.broadcasted_iota(jnp.int32, (panel, points), 0) + part * panel
        chosen = jnp.where(source == wanted, 1.0, 0.0).astype(BF)
        ordered = ordered + jnp.dot(
            raw[:, part * panel : (part + 1) * panel], chosen, preferred_element_type=F32
        )
    own[2] = ordered.astype(BF)
    loads[2].wait()
    loads[3].wait()
    mine = pl.ds(pl.multiple_of(col * panel, panel), panel)
    own_z[col] = own[2, :, mine]

    pl.semaphore_wait(barrier, greeted)

    sent = []

    def send_direct(k):
        for i in range(feats):
            other = peer(i)
            copy = pltpu.make_async_remote_copy(
                src_ref=own.at[:, :, pl.ds(pl.multiple_of(other * panel, panel), panel)],
                dst_ref=slots.at[SLOT[k], col],
                send_sem=slot_send.at[SLOT[k], i],
                recv_sem=slot_recv.at[SLOT[k], col],
                device_id=device(-k, other),
                device_id_type=MESH,
            )
            copy.start()
            sent.append(copy)

    far_first = sorted(DIRECT, key=lambda k: -abs(k))
    for k in far_first:
        send_direct(k)
    for i in range(1, feats):
        other = peer(i)
        copy = pltpu.make_async_remote_copy(
            src_ref=own.at[0:2],
            dst_ref=full.at[col],
            send_sem=full_send.at[i],
            recv_sem=full_recv.at[col],
            device_id=(row, other),
            device_id_type=MESH,
        )
        copy.start()
        sent.append(copy)
        copy = pltpu.make_async_remote_copy(
            src_ref=own.at[2, :, pl.ds(pl.multiple_of(other * panel, panel), panel)],
            dst_ref=own_z.at[col],
            send_sem=z_send.at[i],
            recv_sem=z_recv.at[col],
            device_id=(row, other),
            device_id_type=MESH,
        )
        copy.start()
        sent.append(copy)

    def arrival(k, source):
        return pltpu.make_async_remote_copy(
            src_ref=slots.at[SLOT[k], source],
            dst_ref=slots.at[SLOT[k], source],
            send_sem=slot_send.at[SLOT[k], 0],
            recv_sem=slot_recv.at[SLOT[k], source],
            device_id=(row, peer(1)),
            device_id_type=MESH,
        )

    def wait_and_forward(k):
        for i in range(feats):
            source = peer(i)
            arrival(k, source).wait_recv()
            for further in OFFS:
                by = ROUTE[abs(further)]
                if by == abs(further) or further * k < 0 or abs(further) - by != abs(k):
                    continue
                step = by if k > 0 else -by
                copy = pltpu.make_async_remote_copy(
                    src_ref=slots.at[SLOT[k], source],
                    dst_ref=slots.at[SLOT[further], source],
                    send_sem=slot_send.at[SLOT[further], i],
                    recv_sem=slot_recv.at[SLOT[further], source],
                    device_id=device(-step, col),
                    device_id_type=MESH,
                )
                copy.start()
                sent.append(copy)

    def panel_left(feature_rows):
        squares = jnp.sum(feature_rows * feature_rows, axis=0, keepdims=True) * scale16
        packed = feature_rows.astype(BF)
        one = jnp.ones((1, panel), F32)
        extra = stacked_rows([*split3(squares), one, one, one], panel)
        extra = jnp.concatenate([extra, jnp.zeros((56, panel), F32)], axis=0).astype(BF)
        flat = jnp.concatenate([packed, packed, packed, extra], axis=0)
        return flat.T

    acc_k[...] = jnp.zeros_like(acc_k)
    acc_d[...] = jnp.zeros_like(acc_d)

    def tile(left, z, c):
        lanes = pl.ds(c * width, width)
        x = jnp.dot(left, right[:, lanes], preferred_element_type=F32)
        x = jnp.maximum(x, TINY)
        r = x * lax.rsqrt(x)
        u = jnp.maximum(4.0 - r, 0.0)
        u3 = u * u * u
        kern = (u3 * (u * (r + 1.0))).astype(BF)
        deriv = (u3 * (1.25 * x)).astype(BF)
        return (
            jnp.dot(z, kern, preferred_element_type=F32),
            jnp.dot(z, deriv, preferred_element_type=F32),
        )

    def slot_operands(k):
        values = slots[SLOT[k]].astype(F32)
        features = values[:, 0:2].reshape(64, panel)
        active = jnp.where(mask[0, 4 + k] > 0, 1.0, 0.0)
        z = (values[:, 2].reshape(32, panel) * active).astype(BF)
        return panel_left(features), z

    relays = [k for k in OFFS if any(abs(f) - ROUTE[abs(f)] == abs(k) for f in OFFS)]
    for k in relays:
        wait_and_forward(k)

    for i in range(1, feats):
        source = peer(i)
        pltpu.make_async_remote_copy(
            src_ref=own.at[0:2], dst_ref=full.at[source], send_sem=full_send.at[i],
            recv_sem=full_recv.at[source], device_id=(row, source), device_id_type=MESH,
        ).wait_recv()
        pltpu.make_async_remote_copy(
            src_ref=own_z.at[source], dst_ref=own_z.at[source], send_sem=z_send.at[i],
            recv_sem=z_recv.at[source], device_id=(row, source), device_id_type=MESH,
        ).wait_recv()

    for c in range(points // width):
        lanes = slice(c * width, (c + 1) * width)
        f = full[:, :, :, lanes].astype(F32).reshape(64, width)
        squares = jnp.sum(f * f, axis=0, keepdims=True) * scale16
        one = jnp.ones((1, width), F32)
        extra = stacked_rows([one, one, one, *split3(squares)], width)
        extra = jnp.concatenate([extra, jnp.zeros((56, width), F32)], axis=0)
        high, middle, low = split3(f * (-2.0 * scale16))
        right[:, lanes] = jnp.concatenate([high, middle, low, extra], axis=0).astype(BF)

    def accumulate(pairs):
        for c in range(points // width):
            lanes = pl.ds(c * width, width)
            total_k, total_d = acc_k[:, lanes], acc_d[:, lanes]
            for left, z in pairs:
                add_k, add_d = tile(left, z, c)
                total_k, total_d = total_k + add_k, total_d + add_d
            acc_k[:, lanes], acc_d[:, lanes] = total_k, total_d

    own_features = full[:, :, :, mine].astype(F32).reshape(64, panel)
    own_probes = own_z[...].astype(F32).reshape(32, panel).astype(BF)
    accumulate([(panel_left(own_features), own_probes)])

    waited = set(relays)
    for k in (1, 2, 3):
        for s in (k, -k):
            if s not in waited:
                wait_and_forward(s)
        accumulate([slot_operands(k), slot_operands(-k)])
    for s in (4, -4):
        wait_and_forward(s)
    last = [slot_operands(4), slot_operands(-4)]
    for c in range(points // width):
        lanes = pl.ds(c * width, width)
        total_k, total_d = acc_k[:, lanes], acc_d[:, lanes]
        for left, z in last:
            add_k, add_d = tile(left, z, c)
            total_k, total_d = total_k + add_k, total_d + add_d
        total_k, total_d = total_k * (1.0 / 256.0), total_d * (1.0 / 64.0)
        acc_k[:, lanes], acc_d[:, lanes] = total_k, total_d
        out_s[c, :, 0] = total_k.astype(BF).reshape(feats, 8, width)
        out_s[c, :, 1] = total_d.astype(BF).reshape(feats, 8, width)
        for i in range(1, feats):
            other = peer(i)
            copy = pltpu.make_async_remote_copy(
                src_ref=out_s.at[c, other],
                dst_ref=out_r.at[c, col],
                send_sem=red_send.at[c, i],
                recv_sem=red_recv.at[c, col],
                device_id=(row, other),
                device_id_type=MESH,
            )
            copy.start()
            sent.append(copy)

    probes_here = pl.ds(pl.multiple_of(col * 8, 8), 8)
    for c in range(points // width):
        lanes = pl.ds(c * width, width)
        total_k, total_d = acc_k[probes_here, lanes], acc_d[probes_here, lanes]
        for i in range(1, feats):
            source = peer(i)
            pltpu.make_async_remote_copy(
                src_ref=out_s.at[c, source], dst_ref=out_r.at[c, source], send_sem=red_send.at[c, i],
                recv_sem=red_recv.at[c, source], device_id=(row, source), device_id_type=MESH,
            ).wait_recv()
            total_k = total_k + out_r[c, source, 0].astype(F32)
            total_d = total_d + out_r[c, source, 1].astype(F32)
        out_k[:, lanes], out_d[:, lanes] = total_k, total_d

    for copy in sent:
        copy.wait_send()


def solution(mesh):
    blocks, feats = mesh.shape["rows"], mesh.shape["feat"]

    def body(features, probes, theta, block_mask, order):
        points, width = features.shape
        columns = probes.shape[1]
        panel = points // feats
        chunks = feats
        ft = features.T.reshape(2, width // 2, points)
        pt = probes.T
        any_space = pl.BlockSpec(memory_space=pl.ANY)
        small = pl.BlockSpec(memory_space=pltpu.SMEM)
        vmem = pl.BlockSpec(memory_space=pltpu.VMEM)
        dma = pltpu.SemaphoreType.DMA
        out = jax.ShapeDtypeStruct((columns, points), F32)
        out_k, out_d = pl.pallas_call(
            functools.partial(kernel, blocks, feats),
            out_shape=(out, out),
            in_specs=[any_space, any_space, small, small, any_space],
            out_specs=(vmem, vmem),
            scratch_shapes=[
                pltpu.VMEM((3, 8, points), BF),
                pltpu.VMEM((8, points), BF),
                pltpu.VMEM((1, points), jnp.int32),
                pltpu.VMEM((feats, 2, 8, points), BF),
                pltpu.VMEM((feats, 8, panel), BF),
                pltpu.VMEM((8, feats, 3, 8, panel), BF),
                pltpu.VMEM((256, points), BF),
                pltpu.VMEM((feats * columns, points), F32),
                pltpu.VMEM((feats * columns, points), F32),
                pltpu.VMEM((chunks, feats, 2, 8, points // chunks), BF),
                pltpu.VMEM((chunks, feats, 2, 8, points // chunks), BF),
                dma((4,)),
                dma((feats,)), dma((feats,)), dma((feats,)), dma((feats,)),
                dma((8, feats)), dma((8, feats)),
                dma((chunks, feats)), dma((chunks, feats)),
            ],
            compiler_params=pltpu.CompilerParams(collective_id=0, has_side_effects=True),
        )(ft, pt, theta, block_mask, order)
        return out_k.T, out_d.T

    return jax.shard_map(
        body,
        mesh=mesh,
        in_specs=(P("rows", "feat"), P("rows", "feat"), P(), P("rows", None), P("rows", None)),
        out_specs=(P("rows", "feat"), P("rows", "feat")),
        check_vma=False,
    )
```

time: 139 us -> 41.5 us (0.30)
  starting transfers between devices: 82.5 us -> 0 us
  Pallas kernels: 0 us -> 37.9 us
  blocking collectives: 23.4 us -> 0 us
  matrix products: 19.2 us -> 0 us
  between operations: 6.92 us -> 1.29 us
  local copies, waits for them, and re-layouts: 5.4 us -> 2 us
    ppermute x16 -> x0, starting transfers between devices: 78.8 us -> none  [passed_along(): return lax.ppermute(value, axis, pairs)]
    pallas_call x0 -> x1, Pallas kernels: none -> 37.9 us  [body(): pl.pallas_call(functools.partial(kernel, blocks, feats), out_shape=(out,...]
    dot_general x27 -> x0, matrix products: 19.2 us -> none  [the longest x9 8.17 us: tile_terms(): second = jnp.dot(deriv, panel_probes, preferred_element_type=jnp.float32)]
    all_gather x1 -> x0, blocking collectives: 12.3 us -> none  [body(): own_full = lax.all_gather(features, 'feat', axis=1, tiled=True)]
    all_to_all x1 -> x0, blocking collectives: 11.1 us -> none  [sent_and_summed(): lax.all_to_all(tiles, axis, split_axis=0, concat_axis=0, tiled=True)]
    all_to_all x1 -> x0, starting transfers between devices: 3.69 us -> none  [sent_to_all(): return lax.all_to_all(copies, axis, split_axis=0, concat_axis=0, tiled=True)]
    gather x1 -> x0, local copies, waits for them, and re-layouts: 3.21 us -> none  [body(): ordered_all = jnp.take(all_probes, order[0], axis=0)]
    unnamed x8 -> x4, local copies, waits for them, and re-layouts: 0.02 us -> 2 us
  transfers between devices with their start and end apart: 17 -> 0, of which waited for: 0 -> 0; matrix products, arithmetic and copies ran while one was open for 16% -> 0% of each run, Pallas kernels for 0% -> 0%
where the time goes in v1:
time: 41.5 us; the launch traced here: 41.2 us
  Pallas kernels  37.9 us (91%)
  local copies, waits for them, and re-layouts  2 us (5%)
  between operations  1.29 us (3%)
    pallas_call x1, Pallas kernels, body(): pl.pallas_call(functools.partial(kernel, blocks, feats), out_shape=(out,...  37.9 us
    unnamed x4, local copies, waits for them, and re-layouts  2 us

profile of v1, /device:TPU:1, one launch (start us, length us, event | category | flops | bytes accessed | tf_op | source)
XLA Modules:
  0.0 41.2 jit_solution(16276245951983966455)
XLA Ops:
  1.3 37.9 %shard_map.68 = (f32[8,1024]{1,0:T(8,128)}, f32[8,1024]{1,0:T(8,128)}) custom-call(bf16[2,8,1024]{2,1,0:T(8,128)(2,1)} %bitcast.6, bf16[8,1024]{1,0:T(8,128)(2,1)} %bitcast.9, f32[1]{0:T(128)S(6)} %copy.9.theta, s32[1,9]{1,0:T(1,128)} %mask.1, s32[1,1024]{1,0:T(1,128)} %order.1), custom_call_target="tpu_custom_call" | custom-call | tf_op jit(solution)/shard_map/pallas_call | solution.py:307
  39.2 0.0 copy-start
  39.2 1.4 %copy.10 = f32[1024,8]{0,1:T(8,128)} copy(f32[1024,8]{0,1:T(8,128)} %bitcast.8) | data formatting | bytes 65536
  40.6 0.0 copy-done
  40.6 0.6 %copy.11 = f32[1024,8]{0,1:T(8,128)} copy(f32[1024,8]{0,1:T(8,128)S(1)} %bitcast.7) | data formatting | bytes 65536
Async XLA Ops:
  39.2 1.4 %copy-start = (f32[8,1024]{1,0:T(8,128)S(1)}, f32[8,1024]{1,0:T(8,128)}, u32[]{:S(2)}) copy-start(f32[8,1024]{1,0:T(8,128)} %get-tuple-element.5) | copy-start | bytes 98308

commit v2 on v1

--- a/solution.py
+++ b/solution.py
@@ -10,11 +10,10 @@
 MESH = pl.DeviceIdType.MESH
 BF = jnp.bfloat16
 F32 = jnp.float32
-ROUTE = {1: 1, 2: 2, 3: 1, 4: 2}
 OFFS = (1, -1, 2, -2, 3, -3, 4, -4)
 SLOT = {k: i for i, k in enumerate(OFFS)}
-DIRECT = [k for k in OFFS if ROUTE[abs(k)] == abs(k)]
 TINY = 1e-30
+FAR = ((0, -2), (0, -3), (0, -4), (2, -3), (2, -4))
 
 
 def rounded(value):
@@ -37,9 +36,9 @@
 
 
 def kernel(
-    blocks, feats, ft, pt, theta, mask, order, out_k, out_d,
-    own, raw, order_v, full, own_z, slots, right, acc_k, acc_d, out_s, out_r,
-    load_sem, full_send, full_recv, z_send, z_recv, slot_send, slot_recv, red_send, red_recv,
+    blocks, feats, ft, pt, theta, mask_in, order, out_k, out_d,
+    mask, own, raw, order_v, full, own_z, slots, right, acc_k, acc_d, out_s, out_r,
+    late_in, load_sem, full_send, full_recv, z_send, z_recv, far_sem, slot_send, slot_recv, red_send, red_recv,
 ):
     row = lax.axis_index("rows")
     col = lax.axis_index("feat")
@@ -56,27 +55,42 @@
     def peer(i):
         return lax.rem(col + i, feats)
 
-    barrier = pltpu.get_barrier_semaphore()
-    greeted = 0
-    for i in range(1, feats):
-        pl.semaphore_signal(barrier, inc=1, device_id=(row, peer(i)), device_id_type=MESH)
-        greeted += 1
-    reach = sorted({s * ROUTE[abs(k)] for k in OFFS for s in (1, -1)}, key=abs)
-    for step in reach:
-        for other in range(feats):
-            pl.semaphore_signal(barrier, inc=1, device_id=device(step, other), device_id_type=MESH)
-            greeted += 1
-
     loads = [
         pltpu.make_async_copy(order, order_v, load_sem.at[0]),
         pltpu.make_async_copy(pt, raw, load_sem.at[1]),
         pltpu.make_async_copy(ft, own.at[0:2], load_sem.at[2]),
         pltpu.make_async_copy(ft, full.at[col], load_sem.at[3]),
+        pltpu.make_async_copy(mask_in, mask, load_sem.at[4]),
     ]
     for load in loads:
         load.start()
 
-    scale16 = 16.0 * jnp.exp(jnp.full((1, panel), -2.0 * theta[0], F32))
+    half = blocks // 2
+    place = lax.rem(row, half)
+    lowest, highest = place == 0, place == half - 1
+
+    barrier = pltpu.get_barrier_semaphore()
+
+    def greet(target):
+        pl.semaphore_signal(barrier, inc=1, device_id=target, device_id_type=MESH)
+
+    def greet_block(step):
+        for other in range(feats):
+            greet(device(step, other))
+
+    for i in range(1, feats):
+        greet((row, peer(i)))
+    greet_block(-1)
+    pl.when(jnp.logical_not(highest))(lambda: greet_block(1))
+    for target, k in FAR:
+        pl.when(place == target)(functools.partial(greet_block, k))
+
+    def count(condition):
+        return condition.astype(jnp.int32)
+
+    greeted = (feats - 1) + feats + feats * count(place != 0)
+    for target, k in FAR:
+        greeted = greeted + feats * count(place == half + target + k)
 
     loads[0].wait()
     loads[1].wait()
@@ -89,32 +103,76 @@
             raw[:, part * panel : (part + 1) * panel], chosen, preferred_element_type=F32
         )
     own[2] = ordered.astype(BF)
-    loads[2].wait()
-    loads[3].wait()
+    for load in loads[2:]:
+        load.wait()
+    scale16 = 16.0 * jnp.exp(jnp.full((1, panel), -2.0 * theta[0], F32))
     mine = pl.ds(pl.multiple_of(col * panel, panel), panel)
     own_z[col] = own[2, :, mine]
 
     pl.semaphore_wait(barrier, greeted)
 
+    @pl.when(highest)
+    def _():
+        for other in range(feats):
+            pl.semaphore_signal(late_in, inc=1, device_id=device(1, other), device_id_type=MESH)
+
     sent = []
 
-    def send_direct(k):
+    def direct(k, i):
+        other = peer(i)
+        return pltpu.make_async_remote_copy(
+            src_ref=own.at[:, :, pl.ds(pl.multiple_of(other * panel, panel), panel)],
+            dst_ref=slots.at[SLOT[k], col],
+            send_sem=slot_send.at[SLOT[k], i],
+            recv_sem=slot_recv.at[SLOT[k], col],
+            device_id=device(-k, other),
+            device_id_type=MESH,
+        )
+
+    def forward(k, i):
+        source = peer(i)
+        step = 1 if k > 0 else -1
+        return pltpu.make_async_remote_copy(
+            src_ref=slots.at[SLOT[k - step], source],
+            dst_ref=slots.at[SLOT[k], source],
+            send_sem=slot_send.at[SLOT[k], i],
+            recv_sem=slot_recv.at[SLOT[k], source],
+            device_id=device(-step, col),
+            device_id_type=MESH,
+        )
+
+    def far_send(target, k, i):
+        other = peer(i)
+        return pltpu.make_async_remote_copy(
+            src_ref=own.at[:, :, pl.ds(pl.multiple_of(other * panel, panel), panel)],
+            dst_ref=slots.at[SLOT[k], col],
+            send_sem=far_sem.at[target // 2, i],
+            recv_sem=slot_recv.at[SLOT[k], col],
+            device_id=device(-k, other),
+            device_id_type=MESH,
+        )
+
+    def start_all(make, *which):
         for i in range(feats):
-            other = peer(i)
-            copy = pltpu.make_async_remote_copy(
-                src_ref=own.at[:, :, pl.ds(pl.multiple_of(other * panel, panel), panel)],
-                dst_ref=slots.at[SLOT[k], col],
-                send_sem=slot_send.at[SLOT[k], i],
-                recv_sem=slot_recv.at[SLOT[k], col],
-                device_id=device(-k, other),
-                device_id_type=MESH,
-            )
-            copy.start()
-            sent.append(copy)
-
-    far_first = sorted(DIRECT, key=lambda k: -abs(k))
-    for k in far_first:
-        send_direct(k)
+            make(*which, i).start()
+
+    def wait_all(make, *which):
+        for i in range(feats):
+            make(*which, i).wait_send()
+
+    def forwarded(k):
+        if k > 0:
+            return place != 0
+        far = [half - 1] + [target - 1 for target, slot in FAR if slot == k and target > 0]
+        yes = place != far[0]
+        for other in far[1:]:
+            yes = yes & (place != other)
+        return yes
+
+    start_all(direct, -1)
+    for target, k in FAR:
+        pl.when(place == half + target + k)(functools.partial(start_all, far_send, target, k))
+    pl.when(jnp.logical_not(lowest))(functools.partial(start_all, direct, 1))
     for i in range(1, feats):
         other = peer(i)
         copy = pltpu.make_async_remote_copy(
@@ -149,24 +207,11 @@
         )
 
     def wait_and_forward(k):
+        further = k + (1 if k > 0 else -1)
         for i in range(feats):
-            source = peer(i)
-            arrival(k, source).wait_recv()
-            for further in OFFS:
-                by = ROUTE[abs(further)]
-                if by == abs(further) or further * k < 0 or abs(further) - by != abs(k):
-                    continue
-                step = by if k > 0 else -by
-                copy = pltpu.make_async_remote_copy(
-                    src_ref=slots.at[SLOT[k], source],
-                    dst_ref=slots.at[SLOT[further], source],
-                    send_sem=slot_send.at[SLOT[further], i],
-                    recv_sem=slot_recv.at[SLOT[further], source],
-                    device_id=device(-step, col),
-                    device_id_type=MESH,
-                )
-                copy.start()
-                sent.append(copy)
+            arrival(k, peer(i)).wait_recv()
+            if abs(further) <= 4:
+                pl.when(forwarded(further))(forward(further, i).start)
 
     def panel_left(feature_rows):
         squares = jnp.sum(feature_rows * feature_rows, axis=0, keepdims=True) * scale16
@@ -201,10 +246,14 @@
         z = (values[:, 2].reshape(32, panel) * active).astype(BF)
         return panel_left(features), z
 
-    relays = [k for k in OFFS if any(abs(f) - ROUTE[abs(f)] == abs(k) for f in OFFS)]
-    for k in relays:
+    def take(k):
         wait_and_forward(k)
 
+        @pl.when(place >= k)
+        def _():
+            wait_and_forward(-k)
+
+    take(1)
     for i in range(1, feats):
         source = peer(i)
         pltpu.make_async_remote_copy(
@@ -239,15 +288,26 @@
     own_probes = own_z[...].astype(F32).reshape(32, panel).astype(BF)
     accumulate([(panel_left(own_features), own_probes)])
 
-    waited = set(relays)
-    for k in (1, 2, 3):
-        for s in (k, -k):
-            if s not in waited:
-                wait_and_forward(s)
-        accumulate([slot_operands(k), slot_operands(-k)])
-    for s in (4, -4):
-        wait_and_forward(s)
-    last = [slot_operands(4), slot_operands(-4)]
+    accumulate([slot_operands(1)])
+    for k in (2, 3, 4):
+        take(k)
+        accumulate([slot_operands(k)])
+
+    @pl.when(lowest)
+    def _():
+        pl.semaphore_wait(late_in, feats)
+        start_all(direct, 1)
+        for k in (2, 3, 4):
+            start_all(forward, k)
+
+    for k in (-1, -2, -3, -4):
+        @pl.when(place < -k)
+        def _():
+            wait_and_forward(k)
+
+        if k > -4:
+            accumulate([slot_operands(k)])
+    last = [slot_operands(-4)]
     for c in range(points // width):
         lanes = pl.ds(c * width, width)
         total_k, total_d = acc_k[:, lanes], acc_d[:, lanes]
@@ -287,6 +347,13 @@
 
     for copy in sent:
         copy.wait_send()
+    for k in (1, -1):
+        wait_all(direct, k)
+    for k in (2, 3, 4):
+        wait_all(forward, k)
+        pl.when(forwarded(-k))(functools.partial(wait_all, forward, -k))
+    for target, k in FAR:
+        pl.when(place == half + target + k)(functools.partial(wait_all, far_send, target, k))
 
 
 def solution(mesh):
@@ -299,17 +366,19 @@
         chunks = feats
         ft = features.T.reshape(2, width // 2, points)
         pt = probes.T
-        any_space = pl.BlockSpec(memory_space=pl.ANY)
+        hbm = pl.BlockSpec(memory_space=pltpu.HBM)
         small = pl.BlockSpec(memory_space=pltpu.SMEM)
+        placed = functools.partial(pltpu.with_memory_space_constraint, memory_space=pltpu.HBM)
         vmem = pl.BlockSpec(memory_space=pltpu.VMEM)
         dma = pltpu.SemaphoreType.DMA
         out = jax.ShapeDtypeStruct((columns, points), F32)
         out_k, out_d = pl.pallas_call(
             functools.partial(kernel, blocks, feats),
             out_shape=(out, out),
-            in_specs=[any_space, any_space, small, small, any_space],
+            in_specs=[hbm, hbm, small, hbm, hbm],
             out_specs=(vmem, vmem),
             scratch_shapes=[
+                pltpu.SMEM((1, block_mask.shape[1]), jnp.int32),
                 pltpu.VMEM((3, 8, points), BF),
                 pltpu.VMEM((8, points), BF),
                 pltpu.VMEM((1, points), jnp.int32),
@@ -321,13 +390,16 @@
                 pltpu.VMEM((feats * columns, points), F32),
                 pltpu.VMEM((chunks, feats, 2, 8, points // chunks), BF),
                 pltpu.VMEM((chunks, feats, 2, 8, points // chunks), BF),
-                dma((4,)),
+                pltpu.SemaphoreType.REGULAR,
+                dma((5,)),
                 dma((feats,)), dma((feats,)), dma((feats,)), dma((feats,)),
-                dma((8, feats)), dma((8, feats)),
+                dma((2, feats)), dma((8, feats)), dma((8, feats)),
                 dma((chunks, feats)), dma((chunks, feats)),
             ],
-            compiler_params=pltpu.CompilerParams(collective_id=0, has_side_effects=True),
-        )(ft, pt, theta, block_mask, order)
+            compiler_params=pltpu.CompilerParams(
+                collective_id=0, has_side_effects=True, vmem_limit_bytes=16 << 20
+            ),
+        )(placed(ft), placed(pt), theta, placed(block_mask), placed(order))
         return out_k.T, out_d.T
 
     return jax.shard_map(

time: 41.5 us -> 35.8 us (0.86)
  the two profiles are of different devices: /device:TPU:1 before, /device:TPU:499 now
where the time goes in v2:
time: 35.8 us; the launch traced here: 35.6 us
  Pallas kernels  33.1 us (92%)
  between operations  1.28 us (4%)
  local copies, waits for them, and re-layouts  1.23 us (3%)
    pallas_call x1, Pallas kernels, body(): pl.pallas_call(functools.partial(kernel, blocks, feats), out_shape=(out,...  33.1 us
    unnamed x2, local copies, waits for them, and re-layouts  1.23 us

profile of v2, /device:TPU:499, one launch (start us, length us, event | category | flops | bytes accessed | tf_op | source)
XLA Modules:
  0.0 35.6 jit_solution(9131143997034792876)
XLA Ops:
  1.3 33.1 %shard_map.68 = (f32[8,1024]{1,0:T(8,128)S(1)}, f32[8,1024]{1,0:T(8,128)S(1)}) custom-call(bf16[2,8,1024]{2,1,0:T(8,128)(2,1)} %bitcast.8, bf16[8,1024]{1,0:T(8,128)(2,1)} %bitcast.9, f32[1]{0:T(128)S(6)} %copy.9.theta, s32[1,9]{1,0:T(1,128)} %mask_in.1, s32[1,1024]{1,0:T(1,128)} %order.1), custom_call_target="tpu_custom_call" | custom-call | tf_op jit(solution)/shard_map/pallas_call | solution.py:375
  34.4 0.6 %copy.10 = f32[1024,8]{0,1:T(8,128)} copy(f32[1024,8]{0,1:T(8,128)S(1)} %bitcast.7) | data formatting | bytes 65536
  35.0 0.6 %copy.11 = f32[1024,8]{0,1:T(8,128)} copy(f32[1024,8]{0,1:T(8,128)S(1)} %bitcast.6) | data formatting | bytes 65536

commit v3 on v2

--- a/solution.py
+++ b/solution.py
@@ -13,7 +13,9 @@
 OFFS = (1, -1, 2, -2, 3, -3, 4, -4)
 SLOT = {k: i for i, k in enumerate(OFFS)}
 TINY = 1e-30
-FAR = ((0, -2), (0, -3), (0, -4), (2, -3), (2, -4))
+LATE_GROUPS = ((1, 2), (3,), (4,))
+FAR = ((0, -2), (0, -3), (0, -4), (1, -2), (1, -4), (2, -3), (2, -4), (3, -4))
+UP = ((1, 1), (1, 2), (1, 3), (1, 4), (3, 3), (3, 4))
 
 
 def rounded(value):
@@ -36,9 +38,9 @@
 
 
 def kernel(
-    blocks, feats, ft, pt, theta, mask_in, order, out_k, out_d,
+    blocks, feats, ft, pt, theta, mask_in, order, out,
     mask, own, raw, order_v, full, own_z, slots, right, acc_k, acc_d, out_s, out_r,
-    late_in, load_sem, full_send, full_recv, z_send, z_recv, far_sem, slot_send, slot_recv, red_send, red_recv,
+    late_in, load_sem, full_send, full_recv, z_send, z_recv, far_sem, up_sem, slot_send, slot_recv, red_send, red_recv,
 ):
     row = lax.axis_index("rows")
     col = lax.axis_index("feat")
@@ -111,10 +113,12 @@
 
     pl.semaphore_wait(barrier, greeted)
 
-    @pl.when(highest)
-    def _():
-        for other in range(feats):
-            pl.semaphore_signal(late_in, inc=1, device_id=device(1, other), device_id_type=MESH)
+    ups = sorted({below for below, _ in UP})
+    for below in ups:
+        @pl.when(place == half - below)
+        def _():
+            for other in range(feats):
+                pl.semaphore_signal(late_in, inc=1, device_id=device(below, other), device_id_type=MESH)
 
     sent = []
 
@@ -146,9 +150,26 @@
         return pltpu.make_async_remote_copy(
             src_ref=own.at[:, :, pl.ds(pl.multiple_of(other * panel, panel), panel)],
             dst_ref=slots.at[SLOT[k], col],
-            send_sem=far_sem.at[target // 2, i],
+            send_sem=far_sem.at[target, i],
             recv_sem=slot_recv.at[SLOT[k], col],
             device_id=device(-k, other),
+            device_id_type=MESH,
+        )
+
+    def up_send(below, k, i):
+        other = peer(i)
+        if k == below:
+            source, lanes = col, pl.ds(pl.multiple_of(other * panel, panel), panel)
+            src_ref, target = own.at[:, :, lanes], device(-below, other)
+        else:
+            source = other
+            src_ref, target = slots.at[SLOT[k - below], other], device(-below, col)
+        return pltpu.make_async_remote_copy(
+            src_ref=src_ref,
+            dst_ref=slots.at[SLOT[k], source],
+            send_sem=up_sem.at[UP.index((below, k)), i],
+            recv_sem=slot_recv.at[SLOT[k], source],
+            device_id=target,
             device_id_type=MESH,
         )
 
@@ -162,16 +183,18 @@
 
     def forwarded(k):
         if k > 0:
-            return place != 0
-        far = [half - 1] + [target - 1 for target, slot in FAR if slot == k and target > 0]
+            far = [0] + [half - below + 1 for below, slot in UP if slot == k and below > 1]
+        else:
+            far = [half - 1] + [target - 1 for target, slot in FAR if slot == k and target > 0]
         yes = place != far[0]
         for other in far[1:]:
             yes = yes & (place != other)
         return yes
 
-    start_all(direct, -1)
+    pl.when(highest)(functools.partial(start_all, direct, -1))
     for target, k in FAR:
         pl.when(place == half + target + k)(functools.partial(start_all, far_send, target, k))
+    pl.when(jnp.logical_not(highest))(functools.partial(start_all, direct, -1))
     pl.when(jnp.logical_not(lowest))(functools.partial(start_all, direct, 1))
     for i in range(1, feats):
         other = peer(i)
@@ -239,19 +262,19 @@
             jnp.dot(z, deriv, preferred_element_type=F32),
         )
 
+    upper = count(place >= half // 2)
+
     def slot_operands(k):
-        values = slots[SLOT[k]].astype(F32)
+        near = upper if k > 0 else 1 - upper
+        values = slots[2 * (abs(k) - 1) + near].astype(F32)
         features = values[:, 0:2].reshape(64, panel)
-        active = jnp.where(mask[0, 4 + k] > 0, 1.0, 0.0)
+        active = jnp.where(mask[0, 4 + abs(k) * (1 - 2 * near)] > 0, 1.0, 0.0)
         z = (values[:, 2].reshape(32, panel) * active).astype(BF)
         return panel_left(features), z
 
     def take(k):
-        wait_and_forward(k)
-
-        @pl.when(place >= k)
-        def _():
-            wait_and_forward(-k)
+        pl.when(place + k < half)(functools.partial(wait_and_forward, k))
+        pl.when(place >= k)(functools.partial(wait_and_forward, -k))
 
     take(1)
     for i in range(1, feats):
@@ -295,18 +318,19 @@
 
     @pl.when(lowest)
     def _():
-        pl.semaphore_wait(late_in, feats)
-        start_all(direct, 1)
-        for k in (2, 3, 4):
-            start_all(forward, k)
-
-    for k in (-1, -2, -3, -4):
-        @pl.when(place < -k)
-        def _():
-            wait_and_forward(k)
-
-        if k > -4:
-            accumulate([slot_operands(k)])
+        pl.semaphore_wait(late_in, feats * len(ups))
+        for below, k in UP:
+            start_all(up_send, below, k)
+
+    def take_late(k):
+        pl.when(place + k >= half)(functools.partial(wait_and_forward, k))
+        pl.when(place < k)(functools.partial(wait_and_forward, -k))
+
+    for group in LATE_GROUPS:
+        for k in group:
+            take_late(k)
+        if 4 not in group:
+            accumulate([slot_operands(-k) for k in group])
     last = [slot_operands(-4)]
     for c in range(points // width):
         lanes = pl.ds(c * width, width)
@@ -343,15 +367,20 @@
             ).wait_recv()
             total_k = total_k + out_r[c, source, 0].astype(F32)
             total_d = total_d + out_r[c, source, 1].astype(F32)
-        out_k[:, lanes], out_d[:, lanes] = total_k, total_d
+        out[0, :, lanes], out[1, :, lanes] = total_k, total_d
 
     for copy in sent:
         copy.wait_send()
-    for k in (1, -1):
-        wait_all(direct, k)
-    for k in (2, 3, 4):
-        wait_all(forward, k)
-        pl.when(forwarded(-k))(functools.partial(wait_all, forward, -k))
+    wait_all(direct, -1)
+    pl.when(jnp.logical_not(lowest))(functools.partial(wait_all, direct, 1))
+    for k in (2, 3, 4, -2, -3, -4):
+        pl.when(forwarded(k))(functools.partial(wait_all, forward, k))
+
+    @pl.when(lowest)
+    def _():
+        for below, k in UP:
+            wait_all(up_send, below, k)
+
     for target, k in FAR:
         pl.when(place == half + target + k)(functools.partial(wait_all, far_send, target, k))
 
@@ -371,12 +400,11 @@
         placed = functools.partial(pltpu.with_memory_space_constraint, memory_space=pltpu.HBM)
         vmem = pl.BlockSpec(memory_space=pltpu.VMEM)
         dma = pltpu.SemaphoreType.DMA
-        out = jax.ShapeDtypeStruct((columns, points), F32)
-        out_k, out_d = pl.pallas_call(
+        out = pl.pallas_call(
             functools.partial(kernel, blocks, feats),
-            out_shape=(out, out),
+            out_shape=jax.ShapeDtypeStruct((2, columns, points), F32),
             in_specs=[hbm, hbm, small, hbm, hbm],
-            out_specs=(vmem, vmem),
+            out_specs=vmem,
             scratch_shapes=[
                 pltpu.SMEM((1, block_mask.shape[1]), jnp.int32),
                 pltpu.VMEM((3, 8, points), BF),
@@ -393,14 +421,14 @@
                 pltpu.SemaphoreType.REGULAR,
                 dma((5,)),
                 dma((feats,)), dma((feats,)), dma((feats,)), dma((feats,)),
-                dma((2, feats)), dma((8, feats)), dma((8, feats)),
+                dma((4, feats)), dma((len(UP), feats)), dma((8, feats)), dma((8, feats)),
                 dma((chunks, feats)), dma((chunks, feats)),
             ],
             compiler_params=pltpu.CompilerParams(
                 collective_id=0, has_side_effects=True, vmem_limit_bytes=16 << 20
             ),
         )(placed(ft), placed(pt), theta, placed(block_mask), placed(order))
-        return out_k.T, out_d.T
+        return out[0].T, out[1].T
 
     return jax.shard_map(
         body,

time: 35.8 us -> 34.2 us (0.955)
  the two profiles are of different devices: /device:TPU:499 before, /device:TPU:1 now
where the time goes in v3:
time: 34.2 us; the launch traced here: 33.5 us
  Pallas kernels  31.6 us (92%)
  between operations  1.28 us (4%)
  local copies, waits for them, and re-layouts  0.63 us (2%)
    pallas_call x1, Pallas kernels, body(): pl.pallas_call(functools.partial(kernel, blocks, feats), out_shape=jax.Sh...  31.6 us

profile of v3, /device:TPU:1, one launch (start us, length us, event | category | flops | bytes accessed | tf_op | source)
XLA Modules:
  0.0 33.5 jit_solution(16481770501808096568)
XLA Ops:
  1.3 31.6 %shard_map.68 = f32[2,8,1024]{2,1,0:T(8,128)S(1)} custom-call(bf16[2,8,1024]{2,1,0:T(8,128)(2,1)} %bitcast.12, bf16[8,1024]{1,0:T(8,128)(2,1)} %bitcast.13, f32[1]{0:T(128)S(6)} %copy.7.theta, s32[1,9]{1,0:T(1,128)} %mask_in.1, s32[1,1024]{1,0:T(1,128)} %order.1), custom_call_target="tpu_custom_call" | custom-call | tf_op jit(solution)/shard_map/pallas_call | solution.py:403
  32.9 0.6 %slice_bitcast_fusion = (f32[1024,8]{0,1:T(8,128)}, f32[1024,8]{0,1:T(8,128)}) fusion(f32[2,8,1024]{2,1,0:T(8,128)S(1)} %shard_map.68), kind=kLoop, calls=%fused_computation | loop fusion | bytes 131072 | tf_op jit(solution)/shard_map/transpose | solution.py:431

commit v4 on v3

--- a/solution.py
+++ b/solution.py
@@ -13,8 +13,10 @@
 OFFS = (1, -1, 2, -2, 3, -3, 4, -4)
 SLOT = {k: i for i, k in enumerate(OFFS)}
 TINY = 1e-30
-LATE_GROUPS = ((1, 2), (3,), (4,))
-FAR = ((0, -2), (0, -3), (0, -4), (1, -2), (1, -4), (2, -3), (2, -4), (3, -4))
+LATE_GROUPS = ((1, 2), (3, 4))
+FAR = ((0, -2), (0, -4), (1, -2), (1, -4), (2, -4), (3, -4))
+BACK = ((0, -3), (1, -3), (2, -3))
+GREETED = (*FAR, (0, -3))
 UP = ((1, 1), (1, 2), (1, 3), (1, 4), (3, 3), (3, 4))
 
 
@@ -40,7 +42,7 @@
 def kernel(
     blocks, feats, ft, pt, theta, mask_in, order, out,
     mask, own, raw, order_v, full, own_z, slots, right, acc_k, acc_d, out_s, out_r,
-    late_in, load_sem, full_send, full_recv, z_send, z_recv, far_sem, up_sem, slot_send, slot_recv, red_send, red_recv,
+    late_in, load_sem, full_send, full_recv, z_send, z_recv, far_sem, back_sem, up_sem, slot_send, slot_recv, red_send, red_recv,
 ):
     row = lax.axis_index("rows")
     col = lax.axis_index("feat")
@@ -84,14 +86,14 @@
         greet((row, peer(i)))
     greet_block(-1)
     pl.when(jnp.logical_not(highest))(lambda: greet_block(1))
-    for target, k in FAR:
+    for target, k in GREETED:
         pl.when(place == target)(functools.partial(greet_block, k))
 
     def count(condition):
         return condition.astype(jnp.int32)
 
     greeted = (feats - 1) + feats + feats * count(place != 0)
-    for target, k in FAR:
+    for target, k in GREETED:
         greeted = greeted + feats * count(place == half + target + k)
 
     loads[0].wait()
@@ -173,6 +175,17 @@
             device_id_type=MESH,
         )
 
+    def back(i):
+        source = peer(i)
+        return pltpu.make_async_remote_copy(
+            src_ref=slots.at[SLOT[-4], source],
+            dst_ref=slots.at[SLOT[-3], source],
+            send_sem=back_sem.at[i],
+            recv_sem=slot_recv.at[SLOT[-3], source],
+            device_id=device(-1, col),
+            device_id_type=MESH,
+        )
+
     def start_all(make, *which):
         for i in range(feats):
             make(*which, i).start()
@@ -185,7 +198,7 @@
         if k > 0:
             far = [0] + [half - below + 1 for below, slot in UP if slot == k and below > 1]
         else:
-            far = [half - 1] + [target - 1 for target, slot in FAR if slot == k and target > 0]
+            far = [half - 1] + [target - 1 for target, slot in FAR + BACK if slot == k and target > 0]
         yes = place != far[0]
         for other in far[1:]:
             yes = yes & (place != other)
@@ -248,19 +261,21 @@
     acc_k[...] = jnp.zeros_like(acc_k)
     acc_d[...] = jnp.zeros_like(acc_d)
 
-    def tile(left, z, c):
-        lanes = pl.ds(c * width, width)
-        x = jnp.dot(left, right[:, lanes], preferred_element_type=F32)
+    def distances(left, c):
+        return jnp.dot(left, right[:, pl.ds(c * width, width)], preferred_element_type=F32)
+
+    def profiles(x):
         x = jnp.maximum(x, TINY)
         r = x * lax.rsqrt(x)
         u = jnp.maximum(4.0 - r, 0.0)
         u3 = u * u * u
-        kern = (u3 * (u * (r + 1.0))).astype(BF)
-        deriv = (u3 * (1.25 * x)).astype(BF)
-        return (
-            jnp.dot(z, kern, preferred_element_type=F32),
-            jnp.dot(z, deriv, preferred_element_type=F32),
-        )
+        return (u3 * (u * (r + 1.0))).astype(BF), (u3 * (1.25 * x)).astype(BF)
+
+    def products(z, pair):
+        return tuple(jnp.dot(z, part, preferred_element_type=F32) for part in pair)
+
+    def tile(left, z, c):
+        return products(z, profiles(distances(left, c)))
 
     upper = count(place >= half // 2)
 
@@ -322,21 +337,26 @@
         for below, k in UP:
             start_all(up_send, below, k)
 
+    @pl.when((place > 0) & (place < 4))
+    def _():
+        for i in range(feats):
+            arrival(-4, peer(i)).wait_recv()
+            back(i).start()
+
     def take_late(k):
         pl.when(place + k >= half)(functools.partial(wait_and_forward, k))
-        pl.when(place < k)(functools.partial(wait_and_forward, -k))
-
-    for group in LATE_GROUPS:
+        late = place < k if k < 4 else place == 0
+        pl.when(late)(functools.partial(wait_and_forward, -k))
+
+    for group in LATE_GROUPS[:-1]:
         for k in group:
             take_late(k)
-        if 4 not in group:
-            accumulate([slot_operands(-k) for k in group])
-    last = [slot_operands(-4)]
-    for c in range(points // width):
+        accumulate([slot_operands(-k) for k in group])
+
+    def hand_out(c, parts):
         lanes = pl.ds(c * width, width)
         total_k, total_d = acc_k[:, lanes], acc_d[:, lanes]
-        for left, z in last:
-            add_k, add_d = tile(left, z, c)
+        for add_k, add_d in parts:
             total_k, total_d = total_k + add_k, total_d + add_d
         total_k, total_d = total_k * (1.0 / 256.0), total_d * (1.0 / 64.0)
         acc_k[:, lanes], acc_d[:, lanes] = total_k, total_d
@@ -355,6 +375,20 @@
             copy.start()
             sent.append(copy)
 
+    for k in LATE_GROUPS[-1]:
+        take_late(k)
+    last = [slot_operands(-k) for k in LATE_GROUPS[-1]]
+    chunks = points // width
+    x = {c: [distances(left, c) for left, _ in last] for c in range(min(2, chunks))}
+    pairs = [profiles(part) for part in x.pop(0)]
+    for c in range(chunks):
+        if c + 2 < chunks:
+            x[c + 2] = [distances(left, c + 2) for left, _ in last]
+        parts = [products(z, pair) for (_, z), pair in zip(last, pairs)]
+        if c + 1 < chunks:
+            pairs = [profiles(part) for part in x.pop(c + 1)]
+        hand_out(c, parts)
+
     probes_here = pl.ds(pl.multiple_of(col * 8, 8), 8)
     for c in range(points // width):
         lanes = pl.ds(c * width, width)
@@ -371,6 +405,7 @@
 
     for copy in sent:
         copy.wait_send()
+    pl.when((place > 0) & (place < 4))(functools.partial(wait_all, back))
     wait_all(direct, -1)
     pl.when(jnp.logical_not(lowest))(functools.partial(wait_all, direct, 1))
     for k in (2, 3, 4, -2, -3, -4):
@@ -421,7 +456,7 @@
                 pltpu.SemaphoreType.REGULAR,
                 dma((5,)),
                 dma((feats,)), dma((feats,)), dma((feats,)), dma((feats,)),
-                dma((4, feats)), dma((len(UP), feats)), dma((8, feats)), dma((8, feats)),
+                dma((4, feats)), dma((feats,)), dma((len(UP), feats)), dma((8, feats)), dma((8, feats)),
                 dma((chunks, feats)), dma((chunks, feats)),
             ],
             compiler_params=pltpu.CompilerParams(

time: 34.2 us -> 33 us (0.965); the launches traced: 33.5 us -> 32.8 us
  Pallas kernels: 31.6 us -> 30.9 us
    pallas_call x1, Pallas kernels: 31.6 us -> 30.9 us  [body(): pl.pallas_call(functools.partial(kernel, blocks, feats), out_shape=jax.Sh...]
where the time goes in v4:
time: 33 us; the launch traced here: 32.8 us
  Pallas kernels  30.9 us (94%)
  between operations  1.28 us (4%)
  local copies, waits for them, and re-layouts  0.63 us (2%)
    pallas_call x1, Pallas kernels, body(): pl.pallas_call(functools.partial(kernel, blocks, feats), out_shape=jax.Sh...  30.9 us

profile of v4, /device:TPU:1, one launch (start us, length us, event | category | flops | bytes accessed | tf_op | source)
XLA Modules:
  0.0 32.8 jit_solution(2428107603103386777)
XLA Ops:
  1.3 30.9 %shard_map.68 = f32[2,8,1024]{2,1,0:T(8,128)S(1)} custom-call(bf16[2,8,1024]{2,1,0:T(8,128)(2,1)} %bitcast.12, bf16[8,1024]{1,0:T(8,128)(2,1)} %bitcast.13, f32[1]{0:T(128)S(6)} %copy.7.theta, s32[1,9]{1,0:T(1,128)} %mask_in.1, s32[1,1024]{1,0:T(1,128)} %order.1), custom_call_target="tpu_custom_call" | custom-call | tf_op jit(solution)/shard_map/pallas_call | solution.py:438
  32.2 0.6 %slice_bitcast_fusion = (f32[1024,8]{0,1:T(8,128)}, f32[1024,8]{0,1:T(8,128)}) fusion(f32[2,8,1024]{2,1,0:T(8,128)S(1)} %shard_map.68), kind=kLoop, calls=%fused_computation | loop fusion | bytes 131072 | tf_op jit(solution)/shard_map/transpose | solution.py:466

commit v5 on v4

--- a/solution.py
+++ b/solution.py
@@ -13,7 +13,7 @@
 OFFS = (1, -1, 2, -2, 3, -3, 4, -4)
 SLOT = {k: i for i, k in enumerate(OFFS)}
 TINY = 1e-30
-LATE_GROUPS = ((1, 2), (3, 4))
+LATE_GROUPS = ((1, 2), (4, 3))
 FAR = ((0, -2), (0, -4), (1, -2), (1, -4), (2, -4), (3, -4))
 BACK = ((0, -3), (1, -3), (2, -3))
 GREETED = (*FAR, (0, -3))
@@ -375,11 +375,13 @@
             copy.start()
             sent.append(copy)
 
+    chunks = points // width
+    last, x = [], {c: [] for c in range(min(2, chunks))}
     for k in LATE_GROUPS[-1]:
         take_late(k)
-    last = [slot_operands(-k) for k in LATE_GROUPS[-1]]
-    chunks = points // width
-    x = {c: [distances(left, c) for left, _ in last] for c in range(min(2, chunks))}
+        last.append(slot_operands(-k))
+        for c in x:
+            x[c].append(distances(last[-1][0], c))
     pairs = [profiles(part) for part in x.pop(0)]
     for c in range(chunks):
         if c + 2 < chunks:

time: 33 us -> 32.9 us (level)
  no operation moved by 1% of the time
where the time goes in v5:
time: 32.9 us; the launch traced here: 32.8 us
  Pallas kernels  30.8 us (94%)
  between operations  1.28 us (4%)
  local copies, waits for them, and re-layouts  0.63 us (2%)
    pallas_call x1, Pallas kernels, body(): pl.pallas_call(functools.partial(kernel, blocks, feats), out_shape=jax.Sh...  30.8 us

profile of v5, /device:TPU:1, one launch (start us, length us, event | category | flops | bytes accessed | tf_op | source)
XLA Modules:
  0.0 32.8 jit_solution(15986236885524629597)
XLA Ops:
  1.3 30.8 %shard_map.68 = f32[2,8,1024]{2,1,0:T(8,128)S(1)} custom-call(bf16[2,8,1024]{2,1,0:T(8,128)(2,1)} %bitcast.12, bf16[8,1024]{1,0:T(8,128)(2,1)} %bitcast.13, f32[1]{0:T(128)S(6)} %copy.7.theta, s32[1,9]{1,0:T(1,128)} %mask_in.1, s32[1,1024]{1,0:T(1,128)} %order.1), custom_call_target="tpu_custom_call" | custom-call | tf_op jit(solution)/shard_map/pallas_call | solution.py:440
  32.1 0.6 %slice_bitcast_fusion = (f32[1024,8]{0,1:T(8,128)}, f32[1024,8]{0,1:T(8,128)}) fusion(f32[2,8,1024]{2,1,0:T(8,128)S(1)} %shard_map.68), kind=kLoop, calls=%fused_computation | loop fusion | bytes 131072 | tf_op jit(solution)/shard_map/transpose | solution.py:468
